TPU v7x, 32 devices: a whole 2x2x4 slice. The times are simulated.
32 devices in a mesh: row: 4 (over z), col: 8 (over y, x, core).
Axes of the slice: x: 2, y: 2, z: 4, core: 2. Of those that a mesh axis runs over, the one named last changes fastest.
Arguments:
- rhs: float32 [64, 131072], P(None, ('row', 'col')), may hold values from -6 to 6
- pivots: int32 [4096], replicated, may hold values from 0 to 131071, as said below
- factor: float32 [4096, 4, 8, 128], P('row', None, 'col'), as said below
- diag_inv: float32 [8, 512, 512], P('row'), as said below
Outputs:
- solution: float32 [64, 4, 8, 128], P(None, None, 'col')
Inputs may be any that keep to these rules, and one draw needn't show every extreme that they name: `pivots`: distinct column numbers, the first 4096 entries of a permutation of 0 .. 131071. `factor`: entry (row i, column q) is zero where q >= 512 * (i // 512). `diag_inv`: each block is unit lower triangular.
All inputs are finite; a program needn't handle non-finite values.
Results may differ from a plain program's by a relative error of at most 0.0001.
Values sent between devices are 32-bit elements; how exact they have to be, the bound alone decides.
A program may use at most 64 MiB of HBM per device.

v0:
```python
import jax
import jax.numpy as jnp
from jax import lax
from jax.sharding import PartitionSpec as P


def broadcast(shard, axis, root):
    mine = lax.axis_index(axis) == root
    return lax.psum(jnp.where(mine, shard, jnp.zeros_like(shard)), axis)


def apply_inverse(values, block_inv):
    return lax.dot_general(
        values,
        block_inv,
        (((1,), (1,)), ((), ())),
        precision=lax.Precision.HIGHEST,
        preferred_element_type=jnp.float32,
    )


def per_device(rhs, pivots, factor, diag_inv):
    my_row = lax.axis_index("row")
    my_col = lax.axis_index("col")
    col_count = lax.axis_size("col")
    rhs_count = rhs.shape[0]
    slab_rows = factor.shape[0]
    rounds = factor.shape[1]
    piece_len = factor.shape[3]
    block_len = diag_inv.shape[1]
    pieces = block_len // piece_len
    blocks_here = slab_rows // block_len
    total_blocks = blocks_here * lax.axis_size("row")
    first_column = (my_row * col_count + my_col) * rhs.shape[1]
    source_len = rhs.shape[1]
    located = pivots - first_column
    inside = (located >= 0) & (located < source_len)
    taken = jnp.take(rhs, jnp.clip(located, 0, source_len - 1), axis=1)
    taken = jnp.where(inside[None, :], taken, 0.0)
    permuted = lax.psum_scatter(
        jnp.transpose(
            taken.reshape(rhs_count, blocks_here * lax.axis_size("row"), block_len), (1, 0, 2)
        ),
        "row",
        scatter_dimension=0,
        tiled=True,
    )
    permuted = lax.psum(permuted, "col")
    factor_rows = factor.reshape(slab_rows, rounds * piece_len)

    def advance(number, solved):
        owner_row = number // blocks_here
        local_block = number % blocks_here
        block_rows = lax.dynamic_slice_in_dim(factor_rows, local_block * block_len, block_len, 0)
        partial_value = lax.dot_general(
            solved.reshape(rhs_count, rounds * piece_len),
            block_rows,
            (((1,), (1,)), ((), ())),
            precision=lax.Precision.HIGHEST,
            preferred_element_type=jnp.float32,
        )
        own_rhs = lax.dynamic_index_in_dim(permuted, local_block, 0, keepdims=False)
        block_inv = lax.dynamic_index_in_dim(diag_inv, local_block, 0, keepdims=False)
        summed = lax.psum(partial_value, "col")
        fresh = apply_inverse(own_rhs - summed, block_inv)
        fresh = broadcast(fresh, "row", owner_row)
        first_piece = number * pieces
        offset_piece = (my_col - first_piece) % col_count
        owns = offset_piece < pieces
        which = jnp.clip(offset_piece, 0, pieces - 1)
        local_round = jnp.clip((first_piece + offset_piece) // col_count, 0, rounds - 1)
        piece = lax.dynamic_slice_in_dim(fresh, which * piece_len, piece_len, 1)
        updated = lax.dynamic_update_index_in_dim(solved, piece[:, None, :], local_round, 1)
        return jnp.where(owns, updated, solved)

    start_state = jnp.zeros((rhs_count, rounds, 1, piece_len), jnp.float32)
    return lax.fori_loop(0, total_blocks, advance, start_state)


def solution(mesh):
    return jax.shard_map(
        per_device,
        mesh=mesh,
        in_specs=(P(None, ("row", "col")), P(), P("row", None, "col", None), P("row", None, None)),
        out_specs=P(None, None, "col", None),
        check_vma=False,
    )
```

profile of v0, /device:TPU:0, one launch (start us, length us, event | category | flops | bytes accessed | tf_op | source)
XLA Modules:
  0.0 882.2 jit_solution(17491685887215917001)
XLA Ops:
  8.1 1.8 copy.8
  9.9 14.1 %gather_fusion = f32[4096,64]{1,0:T(8,128)} fusion(f32[64,4096]{0,1:T(8,128)S(1)} %copy.8, s32[4096]{0:T(1024)S(1)} %fusion.8), kind=kCustom, calls=%fused_computation | custom fusion | bytes 2113536 | tf_op jit(solution)/shard_map/jit(_take)/gather | solution.py:38
  24.0 2.2 copy.9
  27.4 30.1 %reduce-scatter.2.cloned.1.call-done = f32[2,64,512]{2,1,0:T(8,128)} async-done(((f32[8,64,512]{2,1,0:T(8,128)}), f32[2,64,512]{2,1,0:T(8,128)}) %reduce-scatter.2.cloned.1.call-update) | async-done | bytes 262160 | tf_op jit(solution)/shard_map/reduce_scatter | solution.py:40
  59.3 53.7 %all-reduce.4.cloned.1.call-done = f32[2,64,512]{2,1,0:T(8,128)} async-done(((f32[2,64,512]{2,1,0:T(8,128)}), f32[2,64,512]{2,1,0:T(8,128)}) %all-reduce.4.cloned.1.call-update) | async-done | bytes 262160 | tf_op jit(solution)/shard_map/psum | solution.py:48
  113.0 761.7 %while.16 = (s32[]{:T(128)}, f32[64,4,1,128]{3,1,0,2:T(4,128)S(1)}, s32[]{:T(128)}, f32[2,64,512]{2,1,0:T(8,128)}, f32[1024,512]{1,0:T(8,128)S(1)}, /*index=5*/f...) while((s32[]{:T(128)}, f32[64,4,1,128]{3,1,0,2:T(4,128)S(1)}, ...), condition=%wide.region_5.6_spmd, body=%wide.region_2.5_spmd.sunk | while | flops 402792448 | bytes 4557184 | solution.py:77
  115.0 54.8 %all-reduce.6.cloned.1.call-done = f32[64,512]{1,0:T(8,128)} async-done(((f32[64,512]{1,0:T(8,128)}), f32[64,512]{1,0:T(8,128)}) %all-reduce.6.cloned.1.call-update) | async-done | bytes 131088 | tf_op jit(solution)/shard_map/while/body/eval_jaxpr/psum | solution.py:64
  169.7 3.1 convolution_select_fusion.2
  172.9 34.1 %all-reduce.8.cloned.1.call-done = f32[64,512]{1,0:T(8,128)} async-done(((f32[64,512]{1,0:T(8,128)}), f32[64,512]{1,0:T(8,128)}) %all-reduce.8.cloned.1.call-update) | async-done | bytes 131088 | tf_op jit(solution)/shard_map/while/body/eval_jaxpr/psum | solution.py:9
  208.1 1.8 convolution_bitcast_fusion.2
  210.0 54.8 %all-reduce.6.cloned.1.call-done = f32[64,512]{1,0:T(8,128)} async-done(((f32[64,512]{1,0:T(8,128)}), f32[64,512]{1,0:T(8,128)}) %all-reduce.6.cloned.1.call-update) | async-done | bytes 131088 | tf_op jit(solution)/shard_map/while/body/eval_jaxpr/psum | solution.py:64
  264.8 3.1 convolution_select_fusion.2
  268.0 34.1 %all-reduce.8.cloned.1.call-done = f32[64,512]{1,0:T(8,128)} async-done(((f32[64,512]{1,0:T(8,128)}), f32[64,512]{1,0:T(8,128)}) %all-reduce.8.cloned.1.call-update) | async-done | bytes 131088 | tf_op jit(solution)/shard_map/while/body/eval_jaxpr/psum | solution.py:9
  305.1 55.1 %all-reduce.6.cloned.1.call-done = f32[64,512]{1,0:T(8,128)} async-done(((f32[64,512]{1,0:T(8,128)}), f32[64,512]{1,0:T(8,128)}) %all-reduce.6.cloned.1.call-update) | async-done | bytes 131088 | tf_op jit(solution)/shard_map/while/body/eval_jaxpr/psum | solution.py:64
  360.1 3.1 convolution_select_fusion.2
  363.3 34.1 %all-reduce.8.cloned.1.call-done = f32[64,512]{1,0:T(8,128)} async-done(((f32[64,512]{1,0:T(8,128)}), f32[64,512]{1,0:T(8,128)}) %all-reduce.8.cloned.1.call-update) | async-done | bytes 131088 | tf_op jit(solution)/shard_map/while/body/eval_jaxpr/psum | solution.py:9
  400.4 55.1 %all-reduce.6.cloned.1.call-done = f32[64,512]{1,0:T(8,128)} async-done(((f32[64,512]{1,0:T(8,128)}), f32[64,512]{1,0:T(8,128)}) %all-reduce.6.cloned.1.call-update) | async-done | bytes 131088 | tf_op jit(solution)/shard_map/while/body/eval_jaxpr/psum | solution.py:64
  455.5 3.1 convolution_select_fusion.2
  458.7 34.1 %all-reduce.8.cloned.1.call-done = f32[64,512]{1,0:T(8,128)} async-done(((f32[64,512]{1,0:T(8,128)}), f32[64,512]{1,0:T(8,128)}) %all-reduce.8.cloned.1.call-update) | async-done | bytes 131088 | tf_op jit(solution)/shard_map/while/body/eval_jaxpr/psum | solution.py:9
  495.8 55.1 %all-reduce.6.cloned.1.call-done = f32[64,512]{1,0:T(8,128)} async-done(((f32[64,512]{1,0:T(8,128)}), f32[64,512]{1,0:T(8,128)}) %all-reduce.6.cloned.1.call-update) | async-done | bytes 131088 | tf_op jit(solution)/shard_map/while/body/eval_jaxpr/psum | solution.py:64
  550.9 3.1 convolution_select_fusion.2
  554.1 34.1 %all-reduce.8.cloned.1.call-done = f32[64,512]{1,0:T(8,128)} async-done(((f32[64,512]{1,0:T(8,128)}), f32[64,512]{1,0:T(8,128)}) %all-reduce.8.cloned.1.call-update) | async-done | bytes 131088 | tf_op jit(solution)/shard_map/while/body/eval_jaxpr/psum | solution.py:9
  589.3 1.8 convolution_bitcast_fusion.2
  591.1 55.1 %all-reduce.6.cloned.1.call-done = f32[64,512]{1,0:T(8,128)} async-done(((f32[64,512]{1,0:T(8,128)}), f32[64,512]{1,0:T(8,128)}) %all-reduce.6.cloned.1.call-update) | async-done | bytes 131088 | tf_op jit(solution)/shard_map/while/body/eval_jaxpr/psum | solution.py:64
  646.2 3.1 convolution_select_fusion.2
  649.4 34.1 %all-reduce.8.cloned.1.call-done = f32[64,512]{1,0:T(8,128)} async-done(((f32[64,512]{1,0:T(8,128)}), f32[64,512]{1,0:T(8,128)}) %all-reduce.8.cloned.1.call-update) | async-done | bytes 131088 | tf_op jit(solution)/shard_map/while/body/eval_jaxpr/psum | solution.py:9
  686.5 54.8 %all-reduce.6.cloned.1.call-done = f32[64,512]{1,0:T(8,128)} async-done(((f32[64,512]{1,0:T(8,128)}), f32[64,512]{1,0:T(8,128)}) %all-reduce.6.cloned.1.call-update) | async-done | bytes 131088 | tf_op jit(solution)/shard_map/while/body/eval_jaxpr/psum | solution.py:64
  741.3 3.1 convolution_select_fusion.2
  744.5 34.1 %all-reduce.8.cloned.1.call-done = f32[64,512]{1,0:T(8,128)} async-done(((f32[64,512]{1,0:T(8,128)}), f32[64,512]{1,0:T(8,128)}) %all-reduce.8.cloned.1.call-update) | async-done | bytes 131088 | tf_op jit(solution)/shard_map/while/body/eval_jaxpr/psum | solution.py:9
  781.6 54.8 %all-reduce.6.cloned.1.call-done = f32[64,512]{1,0:T(8,128)} async-done(((f32[64,512]{1,0:T(8,128)}), f32[64,512]{1,0:T(8,128)}) %all-reduce.6.cloned.1.call-update) | async-done | bytes 131088 | tf_op jit(solution)/shard_map/while/body/eval_jaxpr/psum | solution.py:64
  836.3 3.1 convolution_select_fusion.2
  839.5 34.1 %all-reduce.8.cloned.1.call-done = f32[64,512]{1,0:T(8,128)} async-done(((f32[64,512]{1,0:T(8,128)}), f32[64,512]{1,0:T(8,128)}) %all-reduce.8.cloned.1.call-update) | async-done | bytes 131088 | tf_op jit(solution)/shard_map/while/body/eval_jaxpr/psum | solution.py:9
  (75 shorter events, 24.8 us)
Async XLA Ops:
  6.5 51.0 %reduce-scatter.2.cloned.1.call-start = ((), (), s32[]{:S(2)}) async-start(), calls=%async_computation.1 | async-start | bytes 1310720 | tf_op jit(solution)/shard_map/reduce_scatter | solution.py:40
  27.3 85.6 %all-reduce.4.cloned.1.call-start = ((), (), s32[]{:S(2)}) async-start(), calls=%async_computation.2 | async-start | bytes 524288 | tf_op jit(solution)/shard_map/psum | solution.py:48
  113.0 56.7 %all-reduce.6.cloned.1.call-start = ((), (), s32[]{:S(2)}) async-start(), calls=%async_computation.3 | async-start | bytes 262144 | tf_op jit(solution)/shard_map/while/body/eval_jaxpr/psum | solution.py:64
  114.9 92.2 %all-reduce.8.cloned.1.call-start = ((), (), s32[]{:S(2)}) async-start(), calls=%async_computation.4 | async-start | bytes 262144 | tf_op jit(solution)/shard_map/while/body/eval_jaxpr/psum | solution.py:9
  208.1 56.7 %all-reduce.6.cloned.1.call-start = ((), (), s32[]{:S(2)}) async-start(), calls=%async_computation.3 | async-start | bytes 262144 | tf_op jit(solution)/shard_map/while/body/eval_jaxpr/psum | solution.py:64
  209.9 92.2 %all-reduce.8.cloned.1.call-start = ((), (), s32[]{:S(2)}) async-start(), calls=%async_computation.4 | async-start | bytes 262144 | tf_op jit(solution)/shard_map/while/body/eval_jaxpr/psum | solution.py:9
  303.1 57.0 %all-reduce.6.cloned.1.call-start = ((), (), s32[]{:S(2)}) async-start(), calls=%async_computation.3 | async-start | bytes 262144 | tf_op jit(solution)/shard_map/while/body/eval_jaxpr/psum | solution.py:64
  305.0 92.5 %all-reduce.8.cloned.1.call-start = ((), (), s32[]{:S(2)}) async-start(), calls=%async_computation.4 | async-start | bytes 262144 | tf_op jit(solution)/shard_map/while/body/eval_jaxpr/psum | solution.py:9
  398.5 57.0 %all-reduce.6.cloned.1.call-start = ((), (), s32[]{:S(2)}) async-start(), calls=%async_computation.3 | async-start | bytes 262144 | tf_op jit(solution)/shard_map/while/body/eval_jaxpr/psum | solution.py:64
  400.4 92.5 %all-reduce.8.cloned.1.call-start = ((), (), s32[]{:S(2)}) async-start(), calls=%async_computation.4 | async-start | bytes 262144 | tf_op jit(solution)/shard_map/while/body/eval_jaxpr/psum | solution.py:9
  493.8 57.0 %all-reduce.6.cloned.1.call-start = ((), (), s32[]{:S(2)}) async-start(), calls=%async_computation.3 | async-start | bytes 262144 | tf_op jit(solution)/shard_map/while/body/eval_jaxpr/psum | solution.py:64
  495.7 92.5 %all-reduce.8.cloned.1.call-start = ((), (), s32[]{:S(2)}) async-start(), calls=%async_computation.4 | async-start | bytes 262144 | tf_op jit(solution)/shard_map/while/body/eval_jaxpr/psum | solution.py:9
  589.2 57.0 %all-reduce.6.cloned.1.call-start = ((), (), s32[]{:S(2)}) async-start(), calls=%async_computation.3 | async-start | bytes 262144 | tf_op jit(solution)/shard_map/while/body/eval_jaxpr/psum | solution.py:64
  591.1 92.5 %all-reduce.8.cloned.1.call-start = ((), (), s32[]{:S(2)}) async-start(), calls=%async_computation.4 | async-start | bytes 262144 | tf_op jit(solution)/shard_map/while/body/eval_jaxpr/psum | solution.py:9
  684.6 56.7 %all-reduce.6.cloned.1.call-start = ((), (), s32[]{:S(2)}) async-start(), calls=%async_computation.3 | async-start | bytes 262144 | tf_op jit(solution)/shard_map/while/body/eval_jaxpr/psum | solution.py:64
  686.4 92.2 %all-reduce.8.cloned.1.call-start = ((), (), s32[]{:S(2)}) async-start(), calls=%async_computation.4 | async-start | bytes 262144 | tf_op jit(solution)/shard_map/while/body/eval_jaxpr/psum | solution.py:9
  779.6 56.7 %all-reduce.6.cloned.1.call-start = ((), (), s32[]{:S(2)}) async-start(), calls=%async_computation.3 | async-start | bytes 262144 | tf_op jit(solution)/shard_map/while/body/eval_jaxpr/psum | solution.py:64
  781.5 92.2 %all-reduce.8.cloned.1.call-start = ((), (), s32[]{:S(2)}) async-start(), calls=%async_computation.4 | async-start | bytes 262144 | tf_op jit(solution)/shard_map/while/body/eval_jaxpr/psum | solution.py:9
  874.7 0.7 copy-start
Sparse Core Ops, SparseCore 0:
  27.5 29.9 reduce-scatter.1
  60.5 52.3 all-reduce.3
  116.8 52.8 all-reduce.5
  173.0 34.0 all-reduce.7
  211.6 53.1 all-reduce.5
  268.0 34.0 all-reduce.7
  307.0 53.1 all-reduce.5
  363.4 34.0 all-reduce.7
  402.3 53.1 all-reduce.5
  458.8 34.0 all-reduce.7
  497.7 53.1 all-reduce.5
  554.1 34.0 all-reduce.7
  593.0 53.1 all-reduce.5
  649.5 34.0 all-reduce.7
  688.1 53.1 all-reduce.5
  744.6 34.0 all-reduce.7
  783.2 53.1 all-reduce.5
  839.6 34.0 all-reduce.7
where the time goes:
time: 883 us; the launch traced here: 882 us
  waiting for transfers between devices  796 us (90%)
  matrix products  39.5 us (4%)
  local copies, waits for them, and re-layouts  28 us (3%)
  between operations  13.5 us (2%)
    psum x8, waiting for transfers between devices, advance(): summed = lax.psum(partial_value, 'col')  439 us
    psum x8, waiting for transfers between devices, broadcast(): return lax.psum(jnp.where(mine, shard, jnp.zeros_like(shard)), axis)  273 us
    psum x1, waiting for transfers between devices, per_device(): permuted = lax.psum(permuted, 'col')  53.7 us
    reduce_scatter x1, waiting for transfers between devices, per_device(): lax.psum_scatter(jnp.transpose(taken.reshape(rhs_count, blocks_here * lax...  30.1 us
    dot_general x8, matrix products, apply_inverse(): lax.dot_general(values, block_inv, (((1,), (1,)), ((), ())), precision=la...  25.1 us
  transfers between devices with their start and end apart: 18, of which 18 were waited for; matrix products, arithmetic and copies ran while one was open for 0% of the time, Pallas kernels for 0%

commit v1 on v0

--- a/solution.py
+++ b/solution.py
@@ -6,7 +6,7 @@
 
 def broadcast(shard, axis, root):
     mine = lax.axis_index(axis) == root
-    return lax.psum(jnp.where(mine, shard, jnp.zeros_like(shard)), axis)
+    return jnp.sum(lax.all_gather(jnp.where(mine, shard, jnp.zeros_like(shard)), axis), axis=0)
 
 
 def apply_inverse(values, block_inv):

time: 883 us -> 720 us (0.82)
  waiting for transfers between devices: 796 us -> 526 us
  blocking collectives: 0 us -> 119 us
    psum x8 -> x0, waiting for transfers between devices: 273 us -> none  [broadcast(): return lax.psum(jnp.where(mine, shard, jnp.zeros_like(shard)), axis)]
    all_gather x0 -> x8, blocking collectives: none -> 119 us  [broadcast(): lax.all_gather(jnp.where(mine, shard, jnp.zeros_like(shard)), axis)]
  transfers between devices with their start and end apart: 18 -> 10, of which waited for: 18 -> 10; matrix products, arithmetic and copies ran while one was open for 0% -> 0% of each run, Pallas kernels for 0% -> 0%
where the time goes in v1:
time: 720 us; the launch traced here: 719 us
  waiting for transfers between devices  526 us (73%)
  blocking collectives  119 us (17%)
  matrix products  34.2 us (5%)
  local copies, waits for them, and re-layouts  20.8 us (3%)
  between operations  13.5 us (2%)
    psum x8, waiting for transfers between devices, advance(): summed = lax.psum(partial_value, 'col')  442 us
    all_gather x8, blocking collectives, broadcast(): lax.all_gather(jnp.where(mine, shard, jnp.zeros_like(shard)), axis)  119 us
    psum x1, waiting for transfers between devices, per_device(): permuted = lax.psum(permuted, 'col')  53.7 us
    reduce_scatter x1, waiting for transfers between devices, per_device(): lax.psum_scatter(jnp.transpose(taken.reshape(rhs_count, blocks_here * lax...  30.1 us
    dot_general x8, matrix products, apply_inverse(): lax.dot_general(values, block_inv, (((1,), (1,)), ((), ())), precision=la...  19.8 us
    gather x2, local copies, waits for them, and re-layouts, per_device(): taken = jnp.take(rhs, jnp.clip(located, 0, source_len - 1), axis=1)  16.3 us
    dot_general x8, matrix products, advance(): lax.dot_general(solved.reshape(rhs_count, rounds * piece_len), block_rows...  14.4 us
  transfers between devices with their start and end apart: 10, of which 10 were waited for; matrix products, arithmetic and copies ran while one was open for 0% of the time, Pallas kernels for 0%

profile of v1, /device:TPU:0, one launch (start us, length us, event | category | flops | bytes accessed | tf_op | source)
XLA Modules:
  0.0 718.9 jit_solution(14909030762982771621)
XLA Ops:
  8.1 1.8 copy.5
  9.9 14.2 %gather_fusion = f32[4096,64]{1,0:T(8,128)} fusion(f32[64,4096]{0,1:T(8,128)S(1)} %copy.5, s32[4096]{0:T(1024)S(1)} %fusion.9), kind=kCustom, calls=%fused_computation | custom fusion | bytes 2113536 | tf_op jit(solution)/shard_map/jit(_take)/gather | solution.py:38
  24.0 2.2 copy.6
  27.5 30.1 %reduce-scatter.2.cloned.1.call-done = f32[2,64,512]{2,1,0:T(8,128)} async-done(((f32[8,64,512]{2,1,0:T(8,128)}), f32[2,64,512]{2,1,0:T(8,128)}) %reduce-scatter.2.cloned.1.call-update) | async-done | bytes 262160 | tf_op jit(solution)/shard_map/reduce_scatter | solution.py:40
  59.4 53.7 %all-reduce.3.cloned.1.call-done = f32[2,64,512]{2,1,0:T(8,128)} async-done(((f32[2,64,512]{2,1,0:T(8,128)}), f32[2,64,512]{2,1,0:T(8,128)}) %all-reduce.3.cloned.1.call-update) | async-done | bytes 262160 | tf_op jit(solution)/shard_map/psum | solution.py:48
  113.1 598.3 %while.16 = (s32[]{:T(128)}, f32[64,4,1,128]{3,2,1,0:T(1,128)S(1)}, s32[]{:T(128)}, f32[2,64,512]{2,1,0:T(8,128)}, f32[1024,512]{1,0:T(8,128)S(1)}, /*index=5*/f...) while((s32[]{:T(128)}, f32[64,4,1,128]{3,2,1,0:T(1,128)S(1)}, ...), condition=%wide.region_5.6_spmd, body=%wide.region_2.5_spmd.sunk | while | flops 402858048 | bytes 5015904 | solution.py:77
  115.1 54.8 %all-reduce.5.cloned.1.call-done = f32[64,512]{1,0:T(8,128)} async-done(((f32[64,512]{1,0:T(8,128)}), f32[64,512]{1,0:T(8,128)}) %all-reduce.5.cloned.1.call-update) | async-done | bytes 131088 | tf_op jit(solution)/shard_map/while/body/eval_jaxpr/psum | solution.py:64
  169.9 2.5 convolution_select_fusion.2
  172.3 14.9 %all-gather.2 = f32[256,512]{1,0:T(8,128)S(1)} all-gather(f32[64,512]{1,0:T(8,128)S(1)} %convolution_select_fusion.2), channel_id=2, replica_groups=mesh['row'=4,'col'=8] {'row'}, dimensions={0}, use_global_device_ids=true | all-gather | bytes 655360 | tf_op jit(solution)/shard_map/while/body/eval_jaxpr/all_gather | solution.py:9
  187.5 1.8 convolution_bitcast_fusion.2
  189.4 55.2 %all-reduce.5.cloned.1.call-done = f32[64,512]{1,0:T(8,128)} async-done(((f32[64,512]{1,0:T(8,128)}), f32[64,512]{1,0:T(8,128)}) %all-reduce.5.cloned.1.call-update) | async-done | bytes 131088 | tf_op jit(solution)/shard_map/while/body/eval_jaxpr/psum | solution.py:64
  244.6 2.5 convolution_select_fusion.2
  247.1 14.9 %all-gather.2 = f32[256,512]{1,0:T(8,128)S(1)} all-gather(f32[64,512]{1,0:T(8,128)S(1)} %convolution_select_fusion.2), channel_id=2, replica_groups=mesh['row'=4,'col'=8] {'row'}, dimensions={0}, use_global_device_ids=true | all-gather | bytes 655360 | tf_op jit(solution)/shard_map/while/body/eval_jaxpr/all_gather | solution.py:9
  264.1 55.2 %all-reduce.5.cloned.1.call-done = f32[64,512]{1,0:T(8,128)} async-done(((f32[64,512]{1,0:T(8,128)}), f32[64,512]{1,0:T(8,128)}) %all-reduce.5.cloned.1.call-update) | async-done | bytes 131088 | tf_op jit(solution)/shard_map/while/body/eval_jaxpr/psum | solution.py:64
  319.3 2.5 convolution_select_fusion.2
  321.8 14.9 %all-gather.2 = f32[256,512]{1,0:T(8,128)S(1)} all-gather(f32[64,512]{1,0:T(8,128)S(1)} %convolution_select_fusion.2), channel_id=2, replica_groups=mesh['row'=4,'col'=8] {'row'}, dimensions={0}, use_global_device_ids=true | all-gather | bytes 655360 | tf_op jit(solution)/shard_map/while/body/eval_jaxpr/all_gather | solution.py:9
  336.9 1.8 convolution_bitcast_fusion.2
  338.8 55.2 %all-reduce.5.cloned.1.call-done = f32[64,512]{1,0:T(8,128)} async-done(((f32[64,512]{1,0:T(8,128)}), f32[64,512]{1,0:T(8,128)}) %all-reduce.5.cloned.1.call-update) | async-done | bytes 131088 | tf_op jit(solution)/shard_map/while/body/eval_jaxpr/psum | solution.py:64
  394.1 2.5 convolution_select_fusion.2
  396.5 14.9 %all-gather.2 = f32[256,512]{1,0:T(8,128)S(1)} all-gather(f32[64,512]{1,0:T(8,128)S(1)} %convolution_select_fusion.2), channel_id=2, replica_groups=mesh['row'=4,'col'=8] {'row'}, dimensions={0}, use_global_device_ids=true | all-gather | bytes 655360 | tf_op jit(solution)/shard_map/while/body/eval_jaxpr/all_gather | solution.py:9
  413.6 55.5 %all-reduce.5.cloned.1.call-done = f32[64,512]{1,0:T(8,128)} async-done(((f32[64,512]{1,0:T(8,128)}), f32[64,512]{1,0:T(8,128)}) %all-reduce.5.cloned.1.call-update) | async-done | bytes 131088 | tf_op jit(solution)/shard_map/while/body/eval_jaxpr/psum | solution.py:64
  469.1 2.5 convolution_select_fusion.2
  471.6 14.9 %all-gather.2 = f32[256,512]{1,0:T(8,128)S(1)} all-gather(f32[64,512]{1,0:T(8,128)S(1)} %convolution_select_fusion.2), channel_id=2, replica_groups=mesh['row'=4,'col'=8] {'row'}, dimensions={0}, use_global_device_ids=true | all-gather | bytes 655360 | tf_op jit(solution)/shard_map/while/body/eval_jaxpr/all_gather | solution.py:9
  488.6 55.5 %all-reduce.5.cloned.1.call-done = f32[64,512]{1,0:T(8,128)} async-done(((f32[64,512]{1,0:T(8,128)}), f32[64,512]{1,0:T(8,128)}) %all-reduce.5.cloned.1.call-update) | async-done | bytes 131088 | tf_op jit(solution)/shard_map/while/body/eval_jaxpr/psum | solution.py:64
  544.1 2.5 convolution_select_fusion.2
  546.6 14.9 %all-gather.2 = f32[256,512]{1,0:T(8,128)S(1)} all-gather(f32[64,512]{1,0:T(8,128)S(1)} %convolution_select_fusion.2), channel_id=2, replica_groups=mesh['row'=4,'col'=8] {'row'}, dimensions={0}, use_global_device_ids=true | all-gather | bytes 655360 | tf_op jit(solution)/shard_map/while/body/eval_jaxpr/all_gather | solution.py:9
  563.6 55.5 %all-reduce.5.cloned.1.call-done = f32[64,512]{1,0:T(8,128)} async-done(((f32[64,512]{1,0:T(8,128)}), f32[64,512]{1,0:T(8,128)}) %all-reduce.5.cloned.1.call-update) | async-done | bytes 131088 | tf_op jit(solution)/shard_map/while/body/eval_jaxpr/psum | solution.py:64
  619.2 2.5 convolution_select_fusion.2
  621.6 14.9 %all-gather.2 = f32[256,512]{1,0:T(8,128)S(1)} all-gather(f32[64,512]{1,0:T(8,128)S(1)} %convolution_select_fusion.2), channel_id=2, replica_groups=mesh['row'=4,'col'=8] {'row'}, dimensions={0}, use_global_device_ids=true | all-gather | bytes 655360 | tf_op jit(solution)/shard_map/while/body/eval_jaxpr/all_gather | solution.py:9
  638.7 55.2 %all-reduce.5.cloned.1.call-done = f32[64,512]{1,0:T(8,128)} async-done(((f32[64,512]{1,0:T(8,128)}), f32[64,512]{1,0:T(8,128)}) %all-reduce.5.cloned.1.call-update) | async-done | bytes 131088 | tf_op jit(solution)/shard_map/while/body/eval_jaxpr/psum | solution.py:64
  693.9 2.5 convolution_select_fusion.2
  696.4 14.9 %all-gather.2 = f32[256,512]{1,0:T(8,128)S(1)} all-gather(f32[64,512]{1,0:T(8,128)S(1)} %convolution_select_fusion.2), channel_id=2, replica_groups=mesh['row'=4,'col'=8] {'row'}, dimensions={0}, use_global_device_ids=true | all-gather | bytes 655360 | tf_op jit(solution)/shard_map/while/body/eval_jaxpr/all_gather | solution.py:9
  (59 shorter events, 17.5 us)
Async XLA Ops:
  6.5 51.1 %reduce-scatter.2.cloned.1.call-start = ((), (), s32[]{:S(2)}) async-start(), calls=%async_computation.1 | async-start | bytes 1310720 | tf_op jit(solution)/shard_map/reduce_scatter | solution.py:40
  27.4 85.6 %all-reduce.3.cloned.1.call-start = ((), (), s32[]{:S(2)}) async-start(), calls=%async_computation.2 | async-start | bytes 524288 | tf_op jit(solution)/shard_map/psum | solution.py:48
  113.1 56.7 %all-reduce.5.cloned.1.call-start = ((), (), s32[]{:S(2)}) async-start(), calls=%async_computation.3 | async-start | bytes 262144 | tf_op jit(solution)/shard_map/while/body/eval_jaxpr/psum | solution.py:64
  187.4 57.2 %all-reduce.5.cloned.1.call-start = ((), (), s32[]{:S(2)}) async-start(), calls=%async_computation.3 | async-start | bytes 262144 | tf_op jit(solution)/shard_map/while/body/eval_jaxpr/psum | solution.py:64
  262.1 57.2 %all-reduce.5.cloned.1.call-start = ((), (), s32[]{:S(2)}) async-start(), calls=%async_computation.3 | async-start | bytes 262144 | tf_op jit(solution)/shard_map/while/body/eval_jaxpr/psum | solution.py:64
  336.9 57.2 %all-reduce.5.cloned.1.call-start = ((), (), s32[]{:S(2)}) async-start(), calls=%async_computation.3 | async-start | bytes 262144 | tf_op jit(solution)/shard_map/while/body/eval_jaxpr/psum | solution.py:64
  411.6 57.5 %all-reduce.5.cloned.1.call-start = ((), (), s32[]{:S(2)}) async-start(), calls=%async_computation.3 | async-start | bytes 262144 | tf_op jit(solution)/shard_map/while/body/eval_jaxpr/psum | solution.py:64
  486.7 57.5 %all-reduce.5.cloned.1.call-start = ((), (), s32[]{:S(2)}) async-start(), calls=%async_computation.3 | async-start | bytes 262144 | tf_op jit(solution)/shard_map/while/body/eval_jaxpr/psum | solution.py:64
  561.7 57.5 %all-reduce.5.cloned.1.call-start = ((), (), s32[]{:S(2)}) async-start(), calls=%async_computation.3 | async-start | bytes 262144 | tf_op jit(solution)/shard_map/while/body/eval_jaxpr/psum | solution.py:64
  636.7 57.2 %all-reduce.5.cloned.1.call-start = ((), (), s32[]{:S(2)}) async-start(), calls=%async_computation.3 | async-start | bytes 262144 | tf_op jit(solution)/shard_map/while/body/eval_jaxpr/psum | solution.py:64
  711.5 0.7 copy-start
Sparse Core Ops, SparseCore 0:
  27.6 29.9 reduce-scatter.1
  60.6 52.3 all-reduce.2
  117.0 52.8 all-reduce.4
  190.9 53.5 all-reduce.4
  265.7 53.6 all-reduce.4
  340.4 53.5 all-reduce.4
  415.5 53.5 all-reduce.4
  490.5 53.5 all-reduce.4
  565.5 53.5 all-reduce.4
  640.3 53.5 all-reduce.4
